TPU v7x, 32 devices: a whole 2x2x4 slice. The times are simulated.
32 devices in a mesh: ctx: 4 (over y, x), fsdp: 8 (over z, core).
Axes of the slice: x: 2, y: 2, z: 4, core: 2. Of those that a mesh axis runs over, the one named last changes fastest.
Arguments:
- hidden_in: bfloat16 [8, 512, 2048], P('fsdp', 'ctx'), may hold values from -6 to 6
- block_order: int32 [8, 8], P('fsdp'), may hold values from 0 to 7, each once within a row
- w_query: bfloat16 [2048, 2048], P('fsdp'), may hold values from -0.125 to 0.125
- w_key: bfloat16 [2048, 2048], P('fsdp'), may hold values from -0.125 to 0.125
- w_value: bfloat16 [2048, 2048], P('fsdp'), may hold values from -0.125 to 0.125
- w_output: bfloat16 [2048, 2048], P('fsdp'), may hold values from -0.125 to 0.125
- w_gate: bfloat16 [2048, 8192], P(None, 'fsdp'), may hold values from -0.125 to 0.125
- w_up: bfloat16 [2048, 8192], P(None, 'fsdp'), may hold values from -0.125 to 0.125
- w_down: bfloat16 [8192, 2048], P('fsdp'), may hold values from -0.0625 to 0.0625
- norm_gains: bfloat16 [4, 2048], P(None, 'fsdp'), may hold values from 0.3 to 5.5
- out_grad: bfloat16 [8, 512, 2048], P('fsdp', 'ctx'), may hold values from -6 to 6
Outputs:
- block_out: bfloat16 [8, 512, 2048], P('fsdp', 'ctx')
- input_grad: float32 [8, 512, 2048], P('fsdp', 'ctx')
- grad_query: float32 [2048, 2048], P('fsdp')
- grad_key: float32 [2048, 2048], P('fsdp')
- grad_value: float32 [2048, 2048], P('fsdp')
- grad_output: float32 [2048, 2048], P('fsdp')
- grad_gate: float32 [2048, 8192], P(None, 'fsdp')
- grad_up: float32 [2048, 8192], P(None, 'fsdp')
- grad_down: float32 [8192, 2048], P('fsdp')
- grad_gains: float32 [4, 2048], P(None, 'fsdp')
Inputs may be any that keep to these rules, and one draw needn't show every extreme that they name: `block_order`: each row names every block 0 to 7 once; entry j is the block of that sequence held in rows j * 64 to (j + 1) * 64 - 1.
All inputs are finite; a program needn't handle non-finite values.
Results may differ from a plain program's by a relative error of at most 0.023.
The roundings to bfloat16 on the way count: a program that leaves them out, or rounds other values in their place, can miss the bound.
Values may be sent and summed in bfloat16 or wider, within the bound.
A program may use at most 320 MiB of HBM per device.

v0:
```python
import jax
import jax.numpy as jnp
from jax import lax
from jax.sharding import PartitionSpec as P

HEADS = 16
HEAD_DIM = 128
norm_eps = 1e-06
rope_base = 500000.0
neg_fill = -1e30


def norm_stat(values):
    return lax.rsqrt(jnp.mean(values * values, axis=-1, keepdims=True) + norm_eps)


def norm_back(values, scale, gain, grad_out):
    weighted = grad_out * gain
    grad_values = scale * weighted - values * (scale * scale * scale) * jnp.mean(
        weighted * values, axis=-1, keepdims=True
    )
    grad_gain = jnp.sum(grad_out * (values * scale), axis=0)
    return (grad_values, grad_gain)


def rotate_half(values):
    half_width = values.shape[-1] // 2
    return jnp.concatenate([-values[..., half_width:], values[..., :half_width]], axis=-1)


def rope_tables(positions, width):
    half_width = width // 2
    inverse = rope_base ** (-(jnp.arange(half_width, dtype=jnp.float32) * 2.0) / width)
    angle = positions.astype(jnp.float32)[:, None] * inverse[None, :]
    cosine = jnp.concatenate([jnp.cos(angle), jnp.cos(angle)], axis=-1)
    sine = jnp.concatenate([jnp.sin(angle), jnp.sin(angle)], axis=-1)
    return (cosine[:, None, :], sine[:, None, :])


def apply_rope(values, cosine, sine):
    shaped = values.reshape(values.shape[0], HEADS, HEAD_DIM)
    return shaped * cosine + rotate_half(shaped) * sine


def rope_back(grads, cosine, sine):
    shaped = grads.reshape(grads.shape[0], HEADS, HEAD_DIM)
    return (shaped * cosine - rotate_half(shaped * sine)).reshape(grads.shape)


def shards(
    hidden_in,
    block_order,
    w_query,
    w_key,
    w_value,
    w_output,
    w_gate,
    w_up,
    w_down,
    norm_gains,
    out_grad,
):
    num_rows = hidden_in.shape[1]
    width = hidden_in.shape[2]
    block_rows = num_rows // 2
    seq_rows = num_rows * lax.axis_size("ctx")
    score_scale = HEAD_DIM ** (-0.5)
    tokens_b = hidden_in[0]
    tokens_f = tokens_b.astype(jnp.float32)
    full_query, full_key, full_value, full_output, gains_b = (
        lax.all_gather(w_query, "fsdp", axis=0, tiled=True),
        lax.all_gather(w_key, "fsdp", axis=0, tiled=True),
        lax.all_gather(w_value, "fsdp", axis=0, tiled=True),
        lax.all_gather(w_output, "fsdp", axis=0, tiled=True),
        lax.all_gather(norm_gains, "fsdp", axis=1, tiled=True),
    )
    gains = gains_b.astype(jnp.float32)
    offsets = jnp.arange(block_rows, dtype=jnp.int32)
    all_pos = (block_order[0][:, None] * block_rows + offsets[None, :]).reshape(seq_rows)
    own_pos = lax.dynamic_slice_in_dim(all_pos, lax.axis_index("ctx") * num_rows, num_rows)
    cosine, sine = rope_tables(own_pos, HEAD_DIM)
    query_raw = jnp.dot(tokens_b, full_query, preferred_element_type=jnp.float32)
    key_raw = jnp.dot(tokens_b, full_key, preferred_element_type=jnp.float32)
    query_scale = norm_stat(query_raw)
    key_scale = norm_stat(key_raw)
    query_heads = apply_rope(query_raw * query_scale * gains[0], cosine, sine).astype(jnp.bfloat16)
    key_b = (
        apply_rope(key_raw * key_scale * gains[1], cosine, sine)
        .astype(jnp.bfloat16)
        .reshape(num_rows, width)
    )
    value_b = jnp.dot(tokens_b, full_value, preferred_element_type=jnp.float32).astype(jnp.bfloat16)
    key_all, value_all = (
        lax.all_gather(key_b, "ctx", axis=0, tiled=True),
        lax.all_gather(value_b, "ctx", axis=0, tiled=True),
    )
    query_major = query_heads.transpose(1, 0, 2)
    key_major = key_all.reshape(seq_rows, HEADS, HEAD_DIM).transpose(1, 0, 2)
    value_major = value_all.reshape(seq_rows, HEADS, HEAD_DIM).transpose(1, 0, 2)
    allowed = all_pos[None, :] <= own_pos[:, None]

    def head_scores(query_one, key_one):
        raw_scores = jnp.dot(query_one, key_one.T, preferred_element_type=jnp.float32) * score_scale
        return jnp.where(allowed, raw_scores, neg_fill)

    def head_forward(items):
        query_one, key_one, value_one = items
        scores = head_scores(query_one, key_one)
        peak = jnp.max(scores, axis=-1, keepdims=True)
        expd = jnp.exp(scores - peak)
        denom = jnp.sum(expd, axis=-1, keepdims=True)
        probs = expd / denom
        mixed_one = jnp.dot(
            probs.astype(jnp.bfloat16), value_one, preferred_element_type=jnp.float32
        )
        return (mixed_one, peak + jnp.log(denom))

    mixed_major, log_total = lax.map(head_forward, (query_major, key_major, value_major))
    mixed_b = mixed_major.transpose(1, 0, 2).reshape(num_rows, width).astype(jnp.bfloat16)
    projected = jnp.dot(mixed_b, full_output, preferred_element_type=jnp.float32)
    proj_scale = norm_stat(projected)
    residual = tokens_f + projected * proj_scale * gains[2]
    residual_b = residual.astype(jnp.bfloat16)
    gate_w, up_w, down_w = (w_gate, w_up, w_down)
    mlp_rows_in = lax.all_gather(residual_b, "fsdp", axis=0, tiled=True)
    gate = jnp.dot(mlp_rows_in, gate_w, preferred_element_type=jnp.float32)
    upward = jnp.dot(mlp_rows_in, up_w, preferred_element_type=jnp.float32)
    sigma = jax.nn.sigmoid(gate)
    hidden_b = (gate * sigma * upward).astype(jnp.bfloat16)
    partial_out = jnp.dot(hidden_b, down_w, preferred_element_type=jnp.float32)
    mlp_out = lax.psum_scatter(partial_out, "fsdp", scatter_dimension=0, tiled=True)
    mlp_scale = norm_stat(mlp_out)
    block_out = residual + mlp_out * mlp_scale * gains[3]
    grad_y = out_grad[0].astype(jnp.float32)
    grad_mlp, gain_ff = norm_back(mlp_out, mlp_scale, gains[3], grad_y)
    grad_mlp_b = grad_mlp.astype(jnp.bfloat16)
    grad_rows = lax.all_gather(grad_mlp_b, "fsdp", axis=0, tiled=True)
    grad_hidden = jnp.dot(grad_rows, down_w.T, preferred_element_type=jnp.float32)
    grad_gate_b = (grad_hidden * upward * sigma * (1.0 + gate * (1.0 - sigma))).astype(jnp.bfloat16)
    grad_up_b = (grad_hidden * (gate * sigma)).astype(jnp.bfloat16)
    back_part = jnp.dot(grad_gate_b, gate_w.T, preferred_element_type=jnp.float32) + jnp.dot(
        grad_up_b, up_w.T, preferred_element_type=jnp.float32
    )
    grad_mlp_in = lax.psum_scatter(back_part, "fsdp", scatter_dimension=0, tiled=True)
    gate_grad_own = jnp.dot(mlp_rows_in.T, grad_gate_b, preferred_element_type=jnp.float32)
    up_grad_own = jnp.dot(mlp_rows_in.T, grad_up_b, preferred_element_type=jnp.float32)
    down_grad_own = jnp.dot(hidden_b.T, grad_rows, preferred_element_type=jnp.float32)
    grad_res = grad_y + grad_mlp_in
    grad_proj, gain_attn = norm_back(projected, proj_scale, gains[2], grad_res)
    grad_proj_b = grad_proj.astype(jnp.bfloat16)
    grad_mixed_b = jnp.dot(grad_proj_b, full_output.T, preferred_element_type=jnp.float32).astype(
        jnp.bfloat16
    )
    grad_mixed_major = grad_mixed_b.reshape(num_rows, HEADS, HEAD_DIM).transpose(1, 0, 2)

    def head_backward(items):
        query_one, key_one, value_one, grad_one, total_one = items
        probs_again = jnp.exp(head_scores(query_one, key_one) - total_one)
        grad_probs = jnp.dot(grad_one, value_one.T, preferred_element_type=jnp.float32)
        grad_value_one = jnp.dot(
            probs_again.astype(jnp.bfloat16).T, grad_one, preferred_element_type=jnp.float32
        )
        grad_scores_b = (
            probs_again * (grad_probs - jnp.sum(probs_again * grad_probs, axis=-1, keepdims=True))
        ).astype(jnp.bfloat16)
        grad_query_one = (
            jnp.dot(grad_scores_b, key_one, preferred_element_type=jnp.float32) * score_scale
        )
        grad_key_one = (
            jnp.dot(grad_scores_b.T, query_one, preferred_element_type=jnp.float32) * score_scale
        )
        return (grad_query_one, grad_key_one, grad_value_one)

    grad_query_major, grad_key_major, grad_value_major = lax.map(
        head_backward, (query_major, key_major, value_major, grad_mixed_major, log_total)
    )
    grad_queries = grad_query_major.transpose(1, 0, 2).reshape(num_rows, width)
    grad_key_all = grad_key_major.transpose(1, 0, 2).reshape(seq_rows, width)
    grad_value_all = grad_value_major.transpose(1, 0, 2).reshape(seq_rows, width)
    grad_keys, grad_values = (
        lax.psum_scatter(grad_key_all, "ctx", scatter_dimension=0, tiled=True),
        lax.psum_scatter(grad_value_all, "ctx", scatter_dimension=0, tiled=True),
    )
    grad_value_b = grad_values.astype(jnp.bfloat16)
    grad_key_raw, gain_key = norm_back(
        key_raw, key_scale, gains[1], rope_back(grad_keys, cosine, sine)
    )
    grad_query_raw, gain_query = norm_back(
        query_raw, query_scale, gains[0], rope_back(grad_queries, cosine, sine)
    )
    grad_key_b = grad_key_raw.astype(jnp.bfloat16)
    grad_query_b = grad_query_raw.astype(jnp.bfloat16)
    input_grad = grad_res + jnp.dot(grad_query_b, full_query.T, preferred_element_type=jnp.float32)
    input_grad = input_grad + jnp.dot(grad_key_b, full_key.T, preferred_element_type=jnp.float32)
    input_grad = input_grad + jnp.dot(
        grad_value_b, full_value.T, preferred_element_type=jnp.float32
    )
    stacked_in = jnp.concatenate([grad_query_b, grad_key_b, grad_value_b], axis=1)
    attn_stack = lax.psum_scatter(
        jnp.concatenate(
            [
                jnp.dot(tokens_b.T, stacked_in, preferred_element_type=jnp.float32),
                jnp.dot(mixed_b.T, grad_proj_b, preferred_element_type=jnp.float32),
            ],
            axis=1,
        ).astype(jnp.bfloat16),
        "fsdp",
        scatter_dimension=0,
        tiled=True,
    )
    gain_stack = jnp.stack([gain_query, gain_key, gain_attn, gain_ff], axis=0)
    gain_total = lax.psum(gain_stack, ("ctx", "fsdp"))
    gain_width = gain_total.shape[1] // lax.axis_size("fsdp")
    gain_own = lax.dynamic_slice_in_dim(
        gain_total, lax.axis_index("fsdp") * gain_width, gain_width, 1
    )
    attn_summed, gate_summed, up_summed, down_summed = (
        lax.psum(attn_stack, "ctx").astype(jnp.float32),
        lax.psum(gate_grad_own.astype(jnp.bfloat16), "ctx").astype(jnp.float32),
        lax.psum(up_grad_own.astype(jnp.bfloat16), "ctx").astype(jnp.float32),
        lax.psum(down_grad_own.astype(jnp.bfloat16), "ctx").astype(jnp.float32),
    )
    return (
        block_out.astype(jnp.bfloat16)[None],
        input_grad[None],
        attn_summed[:, :width],
        attn_summed[:, width : 2 * width],
        attn_summed[:, 2 * width : 3 * width],
        attn_summed[:, 3 * width :],
        gate_summed,
        up_summed,
        down_summed,
        gain_own,
    )


def solution(mesh):
    return jax.shard_map(
        shards,
        mesh=mesh,
        in_specs=(
            P("fsdp", "ctx", None),
            P("fsdp", None),
            P("fsdp", None),
            P("fsdp", None),
            P("fsdp", None),
            P("fsdp", None),
            P(None, "fsdp"),
            P(None, "fsdp"),
            P("fsdp", None),
            P(None, "fsdp"),
            P("fsdp", "ctx", None),
        ),
        out_specs=(
            P("fsdp", "ctx", None),
            P("fsdp", "ctx", None),
            P("fsdp", None),
            P("fsdp", None),
            P("fsdp", None),
            P("fsdp", None),
            P(None, "fsdp"),
            P(None, "fsdp"),
            P("fsdp", None),
            P(None, "fsdp"),
        ),
        check_vma=False,
    )
```

profile of v0, /device:TPU:0, one launch (start us, length us, event | category | flops | bytes accessed | tf_op | source)
XLA Modules:
  0.0 1702.8 jit_solution(14575378265479232911)
XLA Ops:
  10.3 14.6 all_gather.28
  25.4 69.0 %all-gather.15.cloned.1.call-done = bf16[2048,2048]{1,0:T(8,128)(2,1)} async-done(((bf16[256,2048]{1,0:T(8,128)(2,1)}), bf16[2048,2048]{1,0:T(8,128)(2,1)}) %all-gather.15.cloned.1.call-update) | async-done | bytes 8388624 | tf_op jit(solution)/shard_map/all_gather | solution.py:73
  94.4 5.4 convolution_convert_fusion.5
  99.9 76.6 %all-gather.11.cloned.1.call-done = bf16[2048,2048]{1,0:T(8,128)(2,1)} async-done(((bf16[256,2048]{1,0:T(8,128)(2,1)}), bf16[2048,2048]{1,0:T(8,128)(2,1)}) %all-gather.11.cloned.1.call-update) | async-done | bytes 8388624 | tf_op jit(solution)/shard_map/all_gather | solution.py:72
  176.5 4.7 multiply_reduce_fusion.8
  184.2 74.4 %all-gather.9.cloned.1.call-done = bf16[2048,2048]{1,0:T(8,128)(2,1)} async-done(((bf16[256,2048]{1,0:T(8,128)(2,1)}), bf16[2048,2048]{1,0:T(8,128)(2,1)}) %all-gather.9.cloned.1.call-update) | async-done | bytes 8388624 | tf_op jit(solution)/shard_map/all_gather | solution.py:71
  258.7 4.8 multiply_reduce_fusion.9
  269.3 25.3 %all-gather.17.cloned.1.call-done = bf16[512,2048]{1,0:T(8,128)(2,1)} async-done(((bf16[128,2048]{1,0:T(8,128)(2,1)}), bf16[512,2048]{1,0:T(8,128)(2,1)}) %all-gather.17.cloned.1.call-update) | async-done | bytes 2097168 | tf_op jit(solution)/shard_map/all_gather | solution.py:95
  294.7 3.5 bitcast_bitcast_fusion
  298.1 34.0 %all-gather.13.cloned.1.call-done = bf16[512,2048]{1,0:T(8,128)(2,1)} async-done(((bf16[128,2048]{1,0:T(8,128)(2,1)}), bf16[512,2048]{1,0:T(8,128)(2,1)}) %all-gather.13.cloned.1.call-update) | async-done | bytes 2097168 | tf_op jit(solution)/shard_map/all_gather | solution.py:94
  332.1 3.5 bitcast_bitcast_fusion.1
  335.6 42.3 %while.28 = (s32[]{:T(128)}, bf16[16,128,128]{1,2,0:T(8,128)(2,1)S(1)}, f32[16,128,1]{1,2,0:T(1,128)S(1)}, bf16[16,128,128]{2,1,0:T(8,128)(2,1)}, bf16[16,512,12...) while((s32[]{:T(128)}, ...), condition=%wide.region_5.6_spmd.clone, body=%wide.region_2.5_spmd.clone.sunk | while | flops 34144128 | bytes 1155689 | solution.py:118
  377.9 37.7 %all-gather.19.cloned.1.call-done = bf16[2048,2048]{1,0:T(8,128)(2,1)} async-done(((bf16[256,2048]{1,0:T(8,128)(2,1)}), bf16[2048,2048]{1,0:T(8,128)(2,1)}) %all-gather.19.cloned.1.call-update) | async-done | bytes 8388624 | tf_op jit(solution)/shard_map/all_gather | solution.py:74
  415.7 4.7 multiply_reduce_fusion.7
  422.7 45.3 %all-gather.21.cloned.1.call-done = bf16[1024,2048]{1,0:T(8,128)(2,1)} async-done(((bf16[128,2048]{1,0:T(8,128)(2,1)}), bf16[1024,2048]{1,0:T(8,128)(2,1)}) %all-gather.21.cloned.1.call-update) | async-done | bytes 4194320 | tf_op jit(solution)/shard_map/all_gather | solution.py:125
  468.0 7.7 fusion.85
  475.7 6.5 multiply_convert_fusion.3
  483.5 6.7 fusion.86
  490.2 88.4 %reduce-scatter.6.cloned.1.call-done = f32[128,2048]{1,0:T(8,128)} async-done(((f32[1024,2048]{1,0:T(8,128)}), f32[128,2048]{1,0:T(8,128)}) %reduce-scatter.6.cloned.1.call-update) | async-done | bytes 1048592 | tf_op jit(solution)/shard_map/reduce_scatter | solution.py:131
  584.4 45.0 %all-gather.23.cloned.1.call-done = bf16[1024,2048]{1,0:T(8,128)(2,1)} async-done(((bf16[128,2048]{1,0:T(8,128)(2,1)}), bf16[1024,2048]{1,0:T(8,128)(2,1)}) %all-gather.23.cloned.1.call-update) | async-done | bytes 4194320 | tf_op jit(solution)/shard_map/all_gather | solution.py:137
  629.5 13.0 multiply_convert_fusion.1
  642.5 7.0 fusion.87
  649.5 6.8 convolution_add_fusion
  656.6 88.3 %reduce-scatter.8.cloned.1.call-done = f32[128,2048]{1,0:T(8,128)} async-done(((f32[1024,2048]{1,0:T(8,128)}), f32[128,2048]{1,0:T(8,128)}) %reduce-scatter.8.cloned.1.call-update) | async-done | bytes 1048592 | tf_op jit(solution)/shard_map/reduce_scatter | solution.py:144
  746.7 3.3 subtract_convert_fusion.2
  750.0 6.5 fusion.56
  757.4 120.4 %while.29 = (s32[]{:T(128)}, f32[16,128,128]{2,1,0:T(8,128)}, f32[16,512,128]{2,1,0:T(8,128)}, f32[16,512,128]{2,1,0:T(8,128)}, bf16[16,128,128]{2,1,0:T(8,128)(...) while((s32[]{:T(128)}, f32[16,128,128]{2,1,0:T(8,128)}, ...), condition=%wide.region_14.15_spmd.clone, body=%wide.region_12.14_spmd.clone.sunk | while | flops 84623232 | bytes 3090561 | solution.py:174
  877.8 4.7 copy_bitcast_fusion.1
  882.6 4.8 copy_bitcast_fusion
  890.2 5.8 convolution_convert_fusion
  897.4 36.3 %reduce-scatter.10.cloned.1.call-done = f32[128,2048]{1,0:T(8,128)} async-done(((f32[512,2048]{1,0:T(8,128)}), f32[128,2048]{1,0:T(8,128)}) %reduce-scatter.10.cloned.1.call-update) | async-done | bytes 1048592 | tf_op jit(solution)/shard_map/reduce_scatter | solution.py:181
  936.8 52.9 %reduce-scatter.12.cloned.1.call-done = f32[128,2048]{1,0:T(8,128)} async-done(((f32[512,2048]{1,0:T(8,128)}), f32[128,2048]{1,0:T(8,128)}) %reduce-scatter.12.cloned.1.call-update) | async-done | bytes 1048592 | tf_op jit(solution)/shard_map/reduce_scatter | solution.py:182
  991.1 11.8 convert_bitcast_fusion
  1002.9 23.9 %pad_maximum_fusion = bf16[2048,8192]{0,1:T(8,128)(2,1)} fusion(bf16[2048,2048]{0,1:T(8,128)(2,1)} %convolution_convert_fusion, bf16[2048,6144]{0,1:T(8,128)(2,1)} %convert_bitcast_fusion), kind=kLoop, calls=%fused_computation.57 | loop fusion | flops 67108864 | bytes 67108864 | tf_op jit(solution)/shard_map/concatenate | solution.py:200
  1027.1 9.6 convolution_convert_fusion.1
  1036.7 6.2 convolution_convert_fusion.2
  1042.9 6.2 convolution_convert_fusion.3
  1049.1 303.3 %reduce-scatter.14.cloned.1.call-done = bf16[256,8192]{0,1:T(8,128)(2,1)} async-done(((bf16[2048,8192]{0,1:T(8,128)(2,1)}), bf16[256,8192]{0,1:T(8,128)(2,1)}) %reduce-scatter.14.cloned.1.call-update) | async-done | bytes 4194320 | tf_op jit(solution)/shard_map/reduce_scatter | solution.py:199
  1353.7 7.2 convolution_add_fusion.3
  1361.0 39.4 %psum.39 = f32[4,2048]{1,0:T(4,128)S(1)} all-reduce(f32[4,2048]{1,0:T(4,128)S(1)} %pad_maximum_fusion.3), channel_id=1, replica_groups=mesh['ctx'=4,'fsdp'=8] {'ctx','fsdp'}, use_global_device_ids=true, to_apply=%region_28.29 | all-reduce | flops 8192 | bytes 65536 | tf_op jit(solution)/shard_map/psum | solution.py:212
  1401.0 6.9 convolution_add_fusion.2
  1407.9 7.3 fusion.48
  1415.2 249.5 %all-reduce.3.cloned.1.call-done = (bf16[256,8192]{0,1:T(8,128)(2,1)}, bf16[2048,1024]{1,0:T(8,128)(2,1)}, bf16[2048,1024]{1,0:T(8,128)(2,1)}, bf16[1024,2048]{1,0:T(8,128)(2,1)}) async-done(((bf16[256,8192]{0,1:T(8,128)(2,1)}, bf16[2048,1024]{1,0:T(8,128)(2,1)}, bf16[2048,1024]{1,0:T(8,128)(2,1)}, bf16[1024,2048]{1,0:T(8,128)(2,1)}), (bf16[256,8192]{0,1:T(8,128)(2,1)}, bf16[2048,1024]{1,0:T(8,128)(2,1)}, ...) | async-done | bytes 16777232 | tf_op jit(solution)/shard_map/psum | solution.py:218
  1664.7 5.0 fusion.82
  1669.7 2.9 copy.59
  1680.2 6.8 convert_element_type.122
  1687.0 4.4 convert_element_type.124
  1691.4 4.4 convert_element_type.126
  (310 shorter events, 205.2 us)
Async XLA Ops:
  7.2 87.2 %copy-start = (bf16[1,128,2048]{2,1,0:T(8,128)(2,1)S(1)}, bf16[1,128,2048]{2,1,0:T(8,128)(2,1)}, u32[]{:S(2)}) copy-start(bf16[1,128,2048]{2,1,0:T(8,128)(2,1)} %param.15) | copy-start | bytes 1572868
  7.2 87.2 %all-gather.15.cloned.1.call-start = ((), (), s32[]{:S(2)}) async-start(), calls=%async_computation.8 | async-start | bytes 9437184 | tf_op jit(solution)/shard_map/all_gather | solution.py:73
  7.9 168.6 %all-gather.11.cloned.1.call-start = ((), (), s32[]{:S(2)}) async-start(), calls=%async_computation.6 | async-start | bytes 9437184 | tf_op jit(solution)/shard_map/all_gather | solution.py:72
  8.7 250.0 %all-gather.9.cloned.1.call-start = ((), (), s32[]{:S(2)}) async-start(), calls=%async_computation.5 | async-start | bytes 9437184 | tf_op jit(solution)/shard_map/all_gather | solution.py:71
  9.4 285.3 %all-gather.17.cloned.1.call-start = ((), (), s32[]{:S(2)}) async-start(), calls=%async_computation.9 | async-start | bytes 2621440 | tf_op jit(solution)/shard_map/all_gather | solution.py:95
  99.8 232.3 %all-gather.13.cloned.1.call-start = ((), (), s32[]{:S(2)}) async-start(), calls=%async_computation.7 | async-start | bytes 2621440 | tf_op jit(solution)/shard_map/all_gather | solution.py:94
  258.7 5.0 copy-start.16
  263.5 1.2 copy-start.15
  266.3 1.0 copy-start.5
  268.7 147.0 %all-gather.19.cloned.1.call-start = ((), (), s32[]{:S(2)}) async-start(), calls=%async_computation.10 | async-start | bytes 9437184 | tf_op jit(solution)/shard_map/all_gather | solution.py:74
  269.3 198.7 %all-gather.21.cloned.1.call-start = ((), (), s32[]{:S(2)}) async-start(), calls=%async_computation.11 | async-start | bytes 4718592 | tf_op jit(solution)/shard_map/all_gather | solution.py:125
  377.9 42.5 %copy-start.10 = (bf16[16,128,128]{1,2,0:T(8,128)(2,1)}, bf16[16,128,128]{1,2,0:T(8,128)(2,1)S(1)}, u32[]{:S(2)}) copy-start(bf16[16,128,128]{1,2,0:T(8,128)(2,1)S(1)} %get-tuple-element.102) | copy-start | bytes 1572868
  420.4 1.0 copy-start.1
  422.4 156.2 %reduce-scatter.6.cloned.1.call-start = ((), (), s32[]{:S(2)}) async-start(), calls=%async_computation.12 | async-start | bytes 9437184 | tf_op jit(solution)/shard_map/reduce_scatter | solution.py:131
  468.0 7.7 copy-start.19
  468.0 7.7 copy-start.21
  475.7 6.5 copy-start.26
  475.7 7.8 copy-start.17
  482.1 1.3 copy-start.23
  490.2 89.9 %copy-start.2 = (bf16[1,128,2048]{2,1,0:T(8,128)(2,1)S(1)}, bf16[1,128,2048]{2,1,0:T(8,128)(2,1)}, u32[]{:S(2)}) copy-start(bf16[1,128,2048]{2,1,0:T(8,128)(2,1)} %param.25) | copy-start | bytes 1572868
  490.2 139.3 %all-gather.23.cloned.1.call-start = ((), (), s32[]{:S(2)}) async-start(), calls=%async_computation.13 | async-start | bytes 4718592 | tf_op jit(solution)/shard_map/all_gather | solution.py:137
  584.0 160.9 %reduce-scatter.8.cloned.1.call-start = ((), (), s32[]{:S(2)}) async-start(), calls=%async_computation.14 | async-start | bytes 9437184 | tf_op jit(solution)/shard_map/reduce_scatter | solution.py:144
  629.5 13.0 copy-start.18
  642.5 7.0 copy-start.24
  642.5 7.0 copy-start.20
  656.3 277.4 %reduce-scatter.10.cloned.1.call-start = ((), (), s32[]{:S(2)}) async-start(), calls=%async_computation.15 | async-start | bytes 5242880 | tf_op jit(solution)/shard_map/reduce_scatter | solution.py:181
  750.0 6.5 copy-start.8
  882.5 107.2 %reduce-scatter.12.cloned.1.call-start = ((), (), s32[]{:S(2)}) async-start(), calls=%async_computation.16 | async-start | bytes 5242880 | tf_op jit(solution)/shard_map/reduce_scatter | solution.py:182
  887.4 465.1 %reduce-scatter.14.cloned.1.call-start = ((), (), s32[]{:S(2)}) async-start(), calls=%async_computation.17 | async-start | bytes 37748736 | tf_op jit(solution)/shard_map/reduce_scatter | solution.py:199
  887.4 1.9 copy-start.3
  889.0 1.1 copy-start.9
  889.0 1.2 copy-start.11
  933.7 1.9 copy-start.6
  933.7 1.9 copy-start.14
  935.6 55.5 %copy-start.7 = (bf16[128,2048]{1,0:T(8,128)(2,1)S(1)}, bf16[128,2048]{1,0:T(8,128)(2,1)}, u32[]{:S(2)}) copy-start(bf16[128,2048]{1,0:T(8,128)(2,1)} %subtract_convert_fusion.1) | copy-start | bytes 1572868
  1026.8 637.9 %all-reduce.3.cloned.1.call-start = ((), (), s32[]{:S(2)}) async-start(), calls=%async_computation.18 | async-start | bytes 33554432 | tf_op jit(solution)/shard_map/psum | solution.py:218
  1027.1 9.6 copy-start.22
  1027.1 9.6 copy-start.25
  1036.7 6.2 copy-start.27
  1352.5 1.2 copy-start.4
  1680.2 6.8 copy-start.13
  1687.0 4.4 copy-start.12
Sparse Core Ops, SparseCore 0:
  9.6 84.7 all-gather.14
  96.0 80.5 all-gather.10
  178.1 80.5 all-gather.8
  261.0 33.6 all-gather.16
  296.9 35.1 all-gather.12
  333.6 82.0 all-gather.18
  422.6 45.3 all-gather.20
  490.3 88.3 reduce-scatter.5
  584.1 45.3 all-gather.22
  656.4 88.3 reduce-scatter.7
  882.6 51.0 reduce-scatter.9
  937.1 52.5 reduce-scatter.11
  1027.0 325.4 reduce-scatter.13
  1357.5 307.2 all-reduce.2
where the time goes:
time: 1720 us; the launch traced here: 1700 us
  waiting for transfers between devices  1230 us (72%)
  matrix products  292 us (17%)
  other arithmetic  69.6 us (4%)
  blocking collectives  54 us (3%)
  local copies, waits for them, and re-layouts  41.3 us (2%)
    reduce_scatter x1, waiting for transfers between devices, shards(): lax.psum_scatter(jnp.concatenate([jnp.dot(tokens_b.T, stacked_in, preferr...  303 us
    psum x1, waiting for transfers between devices, shards(): lax.psum(attn_stack, 'ctx').astype(jnp.float32)  250 us
    reduce_scatter x1, waiting for transfers between devices, shards(): lax.psum_scatter(partial_out, 'fsdp', scatter_dimension=0, tiled=True)  88.4 us
    reduce_scatter x1, waiting for transfers between devices, shards(): lax.psum_scatter(back_part, 'fsdp', scatter_dimension=0, tiled=True)  88.3 us
    all_gather x1, waiting for transfers between devices, shards(): lax.all_gather(w_key, 'fsdp', axis=0, tiled=True)  76.6 us
    all_gather x1, waiting for transfers between devices, shards(): lax.all_gather(w_query, 'fsdp', axis=0, tiled=True)  74.4 us
    all_gather x1, waiting for transfers between devices, shards(): lax.all_gather(w_value, 'fsdp', axis=0, tiled=True)  69 us
    reduce_scatter x1, waiting for transfers between devices, shards(): lax.psum_scatter(grad_value_all, 'ctx', scatter_dimension=0, tiled=True)  52.9 us
  transfers between devices with their start and end apart: 14, of which 14 were waited for; matrix products, arithmetic and copies ran while one was open for 8% of the time, Pallas kernels for 0%

commit v1 on v0

--- a/solution.py
+++ b/solution.py
@@ -209,7 +209,7 @@
         tiled=True,
     )
     gain_stack = jnp.stack([gain_query, gain_key, gain_attn, gain_ff], axis=0)
-    gain_total = lax.psum(gain_stack, ("ctx", "fsdp"))
+    gain_total = jnp.sum(lax.all_gather(gain_stack, ("ctx", "fsdp")), axis=0)
     gain_width = gain_total.shape[1] // lax.axis_size("fsdp")
     gain_own = lax.dynamic_slice_in_dim(
         gain_total, lax.axis_index("fsdp") * gain_width, gain_width, 1

time: 1720 us -> 1770 us (1.029)
  waiting for transfers between devices: 1230 us -> 1320 us
  blocking collectives: 54 us -> 14.6 us
    psum x1, waiting for transfers between devices: 250 us -> 309 us  [shards(): lax.psum(attn_stack, 'ctx').astype(jnp.float32)]
    psum x1 -> x0, blocking collectives: 39.4 us -> none  [shards(): gain_total = lax.psum(gain_stack, ('ctx', 'fsdp'))]
    all_gather x0 -> x1, waiting for transfers between devices: none -> 34.7 us  [shards(): gain_total = jnp.sum(lax.all_gather(gain_stack, ('ctx', 'fsdp')), axis=0)]
  transfers between devices with their start and end apart: 14 -> 15, of which waited for: 14 -> 15; matrix products, arithmetic and copies ran while one was open for 8% -> 8% of each run, Pallas kernels for 0% -> 0%
where the time goes in v1:
time: 1770 us; the launch traced here: 1760 us
  waiting for transfers between devices  1320 us (75%)
  matrix products  290 us (16%)
  other arithmetic  71.6 us (4%)
  local copies, waits for them, and re-layouts  41.6 us (2%)
    psum x1, waiting for transfers between devices, shards(): lax.psum(attn_stack, 'ctx').astype(jnp.float32)  309 us
    reduce_scatter x1, waiting for transfers between devices, shards(): lax.psum_scatter(jnp.concatenate([jnp.dot(tokens_b.T, stacked_in, preferr...  303 us
    reduce_scatter x1, waiting for transfers between devices, shards(): lax.psum_scatter(partial_out, 'fsdp', scatter_dimension=0, tiled=True)  88.4 us
    reduce_scatter x1, waiting for transfers between devices, shards(): lax.psum_scatter(back_part, 'fsdp', scatter_dimension=0, tiled=True)  88.2 us
    all_gather x1, waiting for transfers between devices, shards(): lax.all_gather(w_key, 'fsdp', axis=0, tiled=True)  76.6 us
    all_gather x1, waiting for transfers between devices, shards(): lax.all_gather(w_query, 'fsdp', axis=0, tiled=True)  74.4 us
    all_gather x1, waiting for transfers between devices, shards(): lax.all_gather(w_value, 'fsdp', axis=0, tiled=True)  69 us
    reduce_scatter x1, waiting for transfers between devices, shards(): lax.psum_scatter(grad_value_all, 'ctx', scatter_dimension=0, tiled=True)  52.9 us
  transfers between devices with their start and end apart: 15, of which 15 were waited for; matrix products, arithmetic and copies ran while one was open for 8% of the time, Pallas kernels for 0%

profile of v1, /device:TPU:0, one launch (start us, length us, event | category | flops | bytes accessed | tf_op | source)
XLA Modules:
  0.0 1757.8 jit_solution(15447227320387927742)
XLA Ops:
  10.3 14.6 all_gather.34
  25.4 69.0 %all-gather.18.cloned.1.call-done = bf16[2048,2048]{1,0:T(8,128)(2,1)} async-done(((bf16[256,2048]{1,0:T(8,128)(2,1)}), bf16[2048,2048]{1,0:T(8,128)(2,1)}) %all-gather.18.cloned.1.call-update) | async-done | bytes 8388624 | tf_op jit(solution)/shard_map/all_gather | solution.py:73
  94.4 5.4 convolution_convert_fusion.5
  99.9 76.6 %all-gather.14.cloned.1.call-done = bf16[2048,2048]{1,0:T(8,128)(2,1)} async-done(((bf16[256,2048]{1,0:T(8,128)(2,1)}), bf16[2048,2048]{1,0:T(8,128)(2,1)}) %all-gather.14.cloned.1.call-update) | async-done | bytes 8388624 | tf_op jit(solution)/shard_map/all_gather | solution.py:72
  176.5 4.7 multiply_reduce_fusion.8
  184.2 74.4 %all-gather.12.cloned.1.call-done = bf16[2048,2048]{1,0:T(8,128)(2,1)} async-done(((bf16[256,2048]{1,0:T(8,128)(2,1)}), bf16[2048,2048]{1,0:T(8,128)(2,1)}) %all-gather.12.cloned.1.call-update) | async-done | bytes 8388624 | tf_op jit(solution)/shard_map/all_gather | solution.py:71
  258.7 4.8 multiply_reduce_fusion.9
  269.3 25.3 %all-gather.20.cloned.1.call-done = bf16[512,2048]{1,0:T(8,128)(2,1)} async-done(((bf16[128,2048]{1,0:T(8,128)(2,1)}), bf16[512,2048]{1,0:T(8,128)(2,1)}) %all-gather.20.cloned.1.call-update) | async-done | bytes 2097168 | tf_op jit(solution)/shard_map/all_gather | solution.py:95
  294.7 3.5 bitcast_bitcast_fusion
  298.1 34.0 %all-gather.16.cloned.1.call-done = bf16[512,2048]{1,0:T(8,128)(2,1)} async-done(((bf16[128,2048]{1,0:T(8,128)(2,1)}), bf16[512,2048]{1,0:T(8,128)(2,1)}) %all-gather.16.cloned.1.call-update) | async-done | bytes 2097168 | tf_op jit(solution)/shard_map/all_gather | solution.py:94
  332.1 3.5 bitcast_bitcast_fusion.1
  335.6 42.3 %while.28 = (s32[]{:T(128)}, bf16[16,128,128]{1,2,0:T(8,128)(2,1)S(1)}, f32[16,128,1]{1,2,0:T(1,128)S(1)}, bf16[16,128,128]{2,1,0:T(8,128)(2,1)}, bf16[16,512,12...) while((s32[]{:T(128)}, ...), condition=%wide.region_5.6_spmd.clone, body=%wide.region_2.5_spmd.clone.sunk | while | flops 34144128 | bytes 1155689 | solution.py:118
  377.9 37.7 %all-gather.22.cloned.1.call-done = bf16[2048,2048]{1,0:T(8,128)(2,1)} async-done(((bf16[256,2048]{1,0:T(8,128)(2,1)}), bf16[2048,2048]{1,0:T(8,128)(2,1)}) %all-gather.22.cloned.1.call-update) | async-done | bytes 8388624 | tf_op jit(solution)/shard_map/all_gather | solution.py:74
  415.7 4.7 multiply_reduce_fusion.7
  422.7 45.3 %all-gather.24.cloned.1.call-done = bf16[1024,2048]{1,0:T(8,128)(2,1)} async-done(((bf16[128,2048]{1,0:T(8,128)(2,1)}), bf16[1024,2048]{1,0:T(8,128)(2,1)}) %all-gather.24.cloned.1.call-update) | async-done | bytes 4194320 | tf_op jit(solution)/shard_map/all_gather | solution.py:125
  468.0 7.7 fusion.85
  475.7 6.5 multiply_convert_fusion.3
  483.5 6.7 fusion.86
  490.2 88.4 %reduce-scatter.6.cloned.1.call-done = f32[128,2048]{1,0:T(8,128)} async-done(((f32[1024,2048]{1,0:T(8,128)}), f32[128,2048]{1,0:T(8,128)}) %reduce-scatter.6.cloned.1.call-update) | async-done | bytes 1048592 | tf_op jit(solution)/shard_map/reduce_scatter | solution.py:131
  584.4 45.0 %all-gather.26.cloned.1.call-done = bf16[1024,2048]{1,0:T(8,128)(2,1)} async-done(((bf16[128,2048]{1,0:T(8,128)(2,1)}), bf16[1024,2048]{1,0:T(8,128)(2,1)}) %all-gather.26.cloned.1.call-update) | async-done | bytes 4194320 | tf_op jit(solution)/shard_map/all_gather | solution.py:137
  629.5 13.0 multiply_convert_fusion.1
  642.5 7.0 fusion.87
  649.5 6.8 convolution_add_fusion
  656.6 88.2 %reduce-scatter.8.cloned.1.call-done = f32[128,2048]{1,0:T(8,128)} async-done(((f32[1024,2048]{1,0:T(8,128)}), f32[128,2048]{1,0:T(8,128)}) %reduce-scatter.8.cloned.1.call-update) | async-done | bytes 1048592 | tf_op jit(solution)/shard_map/reduce_scatter | solution.py:144
  746.7 3.3 subtract_convert_fusion.2
  750.0 6.5 fusion.56
  757.4 120.3 %while.29 = (s32[]{:T(128)}, f32[16,128,128]{2,1,0:T(8,128)}, f32[16,512,128]{2,1,0:T(8,128)}, f32[16,512,128]{2,1,0:T(8,128)}, bf16[16,128,128]{2,1,0:T(8,128)(...) while((s32[]{:T(128)}, f32[16,128,128]{2,1,0:T(8,128)}, ...), condition=%wide.region_14.15_spmd.clone, body=%wide.region_12.14_spmd.clone.sunk | while | flops 84623232 | bytes 3090561 | solution.py:174
  877.7 4.7 copy_bitcast_fusion.1
  882.5 4.8 copy_bitcast_fusion
  890.1 5.8 convolution_convert_fusion
  897.4 36.3 %reduce-scatter.10.cloned.1.call-done = f32[128,2048]{1,0:T(8,128)} async-done(((f32[512,2048]{1,0:T(8,128)}), f32[128,2048]{1,0:T(8,128)}) %reduce-scatter.10.cloned.1.call-update) | async-done | bytes 1048592 | tf_op jit(solution)/shard_map/reduce_scatter | solution.py:181
  936.8 52.9 %reduce-scatter.12.cloned.1.call-done = f32[128,2048]{1,0:T(8,128)} async-done(((f32[512,2048]{1,0:T(8,128)}), f32[128,2048]{1,0:T(8,128)}) %reduce-scatter.12.cloned.1.call-update) | async-done | bytes 1048592 | tf_op jit(solution)/shard_map/reduce_scatter | solution.py:182
  991.0 11.8 convert_bitcast_fusion
  1002.8 23.9 %pad_maximum_fusion = bf16[2048,8192]{0,1:T(8,128)(2,1)} fusion(bf16[2048,2048]{0,1:T(8,128)(2,1)} %convolution_convert_fusion, bf16[2048,6144]{0,1:T(8,128)(2,1)} %convert_bitcast_fusion), kind=kLoop, calls=%fused_computation.57 | loop fusion | flops 67108864 | bytes 67108864 | tf_op jit(solution)/shard_map/concatenate | solution.py:200
  1027.7 9.6 convolution_convert_fusion.1
  1037.3 6.2 convolution_convert_fusion.2
  1043.5 6.2 convolution_convert_fusion.3
  1049.8 302.6 %reduce-scatter.14.cloned.1.call-done = bf16[256,8192]{0,1:T(8,128)(2,1)} async-done(((bf16[2048,8192]{0,1:T(8,128)(2,1)}), bf16[256,8192]{0,1:T(8,128)(2,1)}) %reduce-scatter.14.cloned.1.call-update) | async-done | bytes 4194320 | tf_op jit(solution)/shard_map/reduce_scatter | solution.py:199
  1353.6 6.3 convolution_add_fusion.3
  1359.8 6.3 convolution_add_fusion.2
  1366.2 7.3 fusion.48
  1373.4 34.7 %all-gather.28.cloned.1.call-done = f32[32,4,2048]{2,1,0:T(4,128)} async-done(((f32[1,4,2048]{2,1,0:T(4,128)}), f32[32,4,2048]{2,1,0:T(4,128)}) %all-gather.28.cloned.1.call-update) | async-done | bytes 1048592 | tf_op jit(solution)/shard_map/all_gather | solution.py:212
  1410.1 309.4 %all-reduce.3.cloned.1.call-done = (bf16[256,8192]{0,1:T(8,128)(2,1)}, bf16[2048,1024]{1,0:T(8,128)(2,1)}, bf16[2048,1024]{1,0:T(8,128)(2,1)}, bf16[1024,2048]{1,0:T(8,128)(2,1)}) async-done(((bf16[256,8192]{0,1:T(8,128)(2,1)}, bf16[2048,1024]{1,0:T(8,128)(2,1)}, bf16[2048,1024]{1,0:T(8,128)(2,1)}, bf16[1024,2048]{1,0:T(8,128)(2,1)}), (bf16[256,8192]{0,1:T(8,128)(2,1)}, bf16[2048,1024]{1,0:T(8,128)(2,1)}, ...) | async-done | bytes 16777232 | tf_op jit(solution)/shard_map/psum | solution.py:218
  1719.5 5.0 fusion.82
  1724.5 2.9 copy.79
  1735.2 6.8 convert_element_type.122
  1742.0 4.4 convert_element_type.124
  1746.4 4.4 convert_element_type.126
  (313 shorter events, 207.4 us)
Async XLA Ops:
  7.2 87.2 %copy-start = (bf16[1,128,2048]{2,1,0:T(8,128)(2,1)S(1)}, bf16[1,128,2048]{2,1,0:T(8,128)(2,1)}, u32[]{:S(2)}) copy-start(bf16[1,128,2048]{2,1,0:T(8,128)(2,1)} %param.15) | copy-start | bytes 1572868
  7.2 87.2 %all-gather.18.cloned.1.call-start = ((), (), s32[]{:S(2)}) async-start(), calls=%async_computation.8 | async-start | bytes 9437184 | tf_op jit(solution)/shard_map/all_gather | solution.py:73
  7.9 168.6 %all-gather.14.cloned.1.call-start = ((), (), s32[]{:S(2)}) async-start(), calls=%async_computation.6 | async-start | bytes 9437184 | tf_op jit(solution)/shard_map/all_gather | solution.py:72
  8.7 250.0 %all-gather.12.cloned.1.call-start = ((), (), s32[]{:S(2)}) async-start(), calls=%async_computation.5 | async-start | bytes 9437184 | tf_op jit(solution)/shard_map/all_gather | solution.py:71
  9.4 285.3 %all-gather.20.cloned.1.call-start = ((), (), s32[]{:S(2)}) async-start(), calls=%async_computation.9 | async-start | bytes 2621440 | tf_op jit(solution)/shard_map/all_gather | solution.py:95
  99.8 232.3 %all-gather.16.cloned.1.call-start = ((), (), s32[]{:S(2)}) async-start(), calls=%async_computation.7 | async-start | bytes 2621440 | tf_op jit(solution)/shard_map/all_gather | solution.py:94
  258.7 5.0 copy-start.16
  263.5 1.2 copy-start.15
  266.3 1.0 copy-start.5
  268.7 147.0 %all-gather.22.cloned.1.call-start = ((), (), s32[]{:S(2)}) async-start(), calls=%async_computation.10 | async-start | bytes 9437184 | tf_op jit(solution)/shard_map/all_gather | solution.py:74
  269.3 198.7 %all-gather.24.cloned.1.call-start = ((), (), s32[]{:S(2)}) async-start(), calls=%async_computation.11 | async-start | bytes 4718592 | tf_op jit(solution)/shard_map/all_gather | solution.py:125
  377.9 42.5 %copy-start.10 = (bf16[16,128,128]{1,2,0:T(8,128)(2,1)}, bf16[16,128,128]{1,2,0:T(8,128)(2,1)S(1)}, u32[]{:S(2)}) copy-start(bf16[16,128,128]{1,2,0:T(8,128)(2,1)S(1)} %get-tuple-element.102) | copy-start | bytes 1572868
  420.4 1.0 copy-start.1
  422.4 156.2 %reduce-scatter.6.cloned.1.call-start = ((), (), s32[]{:S(2)}) async-start(), calls=%async_computation.12 | async-start | bytes 9437184 | tf_op jit(solution)/shard_map/reduce_scatter | solution.py:131
  468.0 7.7 copy-start.19
  468.0 7.7 copy-start.21
  475.7 6.5 copy-start.26
  475.7 7.8 copy-start.17
  482.1 1.3 copy-start.23
  490.2 89.9 %copy-start.2 = (bf16[1,128,2048]{2,1,0:T(8,128)(2,1)S(1)}, bf16[1,128,2048]{2,1,0:T(8,128)(2,1)}, u32[]{:S(2)}) copy-start(bf16[1,128,2048]{2,1,0:T(8,128)(2,1)} %param.25) | copy-start | bytes 1572868
  490.2 139.3 %all-gather.26.cloned.1.call-start = ((), (), s32[]{:S(2)}) async-start(), calls=%async_computation.13 | async-start | bytes 4718592 | tf_op jit(solution)/shard_map/all_gather | solution.py:137
  584.0 160.8 %reduce-scatter.8.cloned.1.call-start = ((), (), s32[]{:S(2)}) async-start(), calls=%async_computation.14 | async-start | bytes 9437184 | tf_op jit(solution)/shard_map/reduce_scatter | solution.py:144
  629.5 13.0 copy-start.18
  642.5 7.0 copy-start.24
  642.5 7.0 copy-start.20
  656.3 277.3 %reduce-scatter.10.cloned.1.call-start = ((), (), s32[]{:S(2)}) async-start(), calls=%async_computation.15 | async-start | bytes 5242880 | tf_op jit(solution)/shard_map/reduce_scatter | solution.py:181
  750.0 6.5 copy-start.8
  882.4 107.2 %reduce-scatter.12.cloned.1.call-start = ((), (), s32[]{:S(2)}) async-start(), calls=%async_computation.16 | async-start | bytes 5242880 | tf_op jit(solution)/shard_map/reduce_scatter | solution.py:182
  887.3 465.0 %reduce-scatter.14.cloned.1.call-start = ((), (), s32[]{:S(2)}) async-start(), calls=%async_computation.17 | async-start | bytes 37748736 | tf_op jit(solution)/shard_map/reduce_scatter | solution.py:199
  887.3 1.9 copy-start.3
  888.9 1.1 copy-start.9
  888.9 1.2 copy-start.11
  933.6 1.9 copy-start.6
  933.6 1.9 copy-start.14
  935.5 55.4 %copy-start.7 = (bf16[128,2048]{1,0:T(8,128)(2,1)S(1)}, bf16[128,2048]{1,0:T(8,128)(2,1)}, u32[]{:S(2)}) copy-start(bf16[128,2048]{1,0:T(8,128)(2,1)} %subtract_convert_fusion.1) | copy-start | bytes 1572868
  1026.7 381.4 %all-gather.28.cloned.1.call-start = ((), (), s32[]{:S(2)}) async-start(), calls=%async_computation.18 | async-start | bytes 1081344 | tf_op jit(solution)/shard_map/all_gather | solution.py:212
  1027.5 692.0 %all-reduce.3.cloned.1.call-start = ((), (), s32[]{:S(2)}) async-start(), calls=%async_computation.19 | async-start | bytes 33554432 | tf_op jit(solution)/shard_map/psum | solution.py:218
  1027.7 9.6 copy-start.22
  1027.7 9.6 copy-start.25
  1037.3 6.2 copy-start.27
  1352.3 1.2 copy-start.4
  1735.2 6.8 copy-start.13
  1742.0 4.4 copy-start.12
Sparse Core Ops, SparseCore 0:
  9.6 84.7 all-gather.17
  96.0 80.5 all-gather.13
  178.1 80.5 all-gather.11
  261.0 33.6 all-gather.19
  296.9 35.1 all-gather.15
  333.6 82.0 all-gather.21
  422.6 45.3 all-gather.23
  490.3 88.3 reduce-scatter.5
  584.1 45.3 all-gather.25
  656.4 88.3 reduce-scatter.7
  882.6 51.0 reduce-scatter.9
  937.0 52.5 reduce-scatter.11
  1026.8 325.4 reduce-scatter.13
  1355.8 52.2 all-gather.27
  1413.1 306.3 all-reduce.2
